TPU v7x, 8 devices: a whole 2x2x1 slice. The times are simulated.
8 devices in a mesh: member: 2 (over z, y), lat: 4 (over x, core).
Axes of the slice: x: 2, y: 2, z: 1, core: 2. Of those that a mesh axis runs over, the one named last changes fastest.
Arguments:
- field_in: float32 [24, 128, 128, 256], P('member', None, 'lat'), parts along dimension 0
- grad_out: float32 [24, 128, 128, 256], P('member', None, 'lat'), parts along dimension 0
- p_fwd: float32 [128, 128, 128], replicated
- p_inv: float32 [128, 128, 128], replicated
- w_mix: float32 [128, 128, 128, 2], replicated
Outputs:
- output 1: float32 [24, 128, 128, 256], P('member', None, 'lat'), parts along dimension 0
- output 2: float32 [256, 128, 128, 2], P('member'), parts along dimension 0
There are 2 independent parts. A program takes and returns all parts, laid end to end along the dimension named above; an argument that names none is the same for every part.
All inputs are finite; a program needn't handle non-finite values.
Results may differ from a plain program's by a relative error of at most 0.00656286.
Values are sent between devices in bfloat16 or wider.
A program may use at most 1 GiB of HBM per device.

v0:
```python
import math
import jax
import jax.numpy as jnp
from jax import lax
from jax.sharding import PartitionSpec as P


def gelu_grad(values):
    cumulative = 0.5 * (1.0 + lax.erf(values * math.sqrt(0.5)))
    density = jnp.exp(-0.5 * values * values) / math.sqrt(2.0 * math.pi)
    return cumulative + values * density


def mix_matrix(w_mix):
    w_real = w_mix[..., 0]
    w_imag = w_mix[..., 1]
    upper_half = jnp.stack([w_real, -w_imag], axis=-1)
    lower_half = jnp.stack([w_imag, w_real], axis=-1)
    return jnp.stack([upper_half, lower_half], axis=2).astype(jnp.bfloat16)


def analysis(values, mode_count, mode_gains):
    spectrum = jnp.fft.rfft(values, axis=-1)[..., :mode_count] * mode_gains
    return jnp.stack([spectrum.real, spectrum.imag], axis=-2).astype(jnp.bfloat16)


def synthesis(spec_pair, lon_count, mode_gains):
    complex_spec = lax.complex(spec_pair[..., 0, :].astype(jnp.float32), spec_pair[..., 1, :].astype(jnp.float32)) * mode_gains
    pad_width = [(0, 0)] * (complex_spec.ndim - 1) + [(0, lon_count // 2 + 1 - complex_spec.shape[-1])]
    return jnp.fft.irfft(jnp.pad(complex_spec, pad_width), n=lon_count, axis=-1)


def solution(mesh):
    lat_size = mesh.shape['lat']
    field_spec = P('member', None, 'lat', None)

    def local_step(field_loc, grad_loc, p_fwd, p_inv, w_mix):
        lon_count = field_loc.shape[-1]
        lat_count = p_fwd.shape[-1]
        m_local = lat_count // lat_size
        m_start = lax.axis_index('lat') * m_local
        root_lon = math.sqrt(lon_count)
        is_mean = jnp.arange(lat_count) == 0
        pw_own = lax.dynamic_slice_in_dim(p_fwd, m_start, m_local, axis=0).astype(jnp.bfloat16)
        pi_own = lax.dynamic_slice_in_dim(p_inv, m_start, m_local, axis=0).astype(jnp.bfloat16)
        w_big = mix_matrix(w_mix)
        four_lat = analysis(field_loc, lat_count, 1.0 / root_lon)
        four_own = lax.all_to_all(four_lat, 'lat', 4, 2, tiled=True)
        coeffs = jnp.einsum('mlt,bctrm->bclrm', pw_own, four_own, preferred_element_type=jnp.float32).astype(jnp.bfloat16)
        mixed_coef = jnp.einsum('losir,bilrm->bolsm', w_big, coeffs, preferred_element_type=jnp.float32).astype(jnp.bfloat16)
        back_own = jnp.einsum('mlt,bclrm->bctrm', pi_own, mixed_coef, preferred_element_type=jnp.float32).astype(jnp.bfloat16)
        back_lat = lax.all_to_all(back_own, 'lat', 2, 4, tiled=True)
        hidden = synthesis(back_lat, lon_count, root_lon)
        grad_hidden = grad_loc * gelu_grad(hidden)
        grad_back_lat = analysis(grad_hidden, lat_count, jnp.where(is_mean, 1.0, 2.0) / root_lon)
        grad_back_own = lax.all_to_all(grad_back_lat, 'lat', 4, 2, tiled=True)
        grad_mixed = jnp.einsum('mlt,bctrm->bclrm', pi_own, grad_back_own, preferred_element_type=jnp.float32).astype(jnp.bfloat16)
        gw_part = jnp.einsum('bolsm,bilrm->losir', grad_mixed, coeffs, preferred_element_type=jnp.float32)
        gw_total = lax.psum(gw_part, 'lat')
        grad_coef = jnp.einsum('losir,bolsm->bilrm', w_big, grad_mixed, preferred_element_type=jnp.float32).astype(jnp.bfloat16)
        grad_four_own = jnp.einsum('mlt,bclrm->bctrm', pw_own, grad_coef, preferred_element_type=jnp.float32).astype(jnp.bfloat16)
        grad_four_lat = lax.all_to_all(grad_four_own, 'lat', 2, 4, tiled=True)
        grad_field = grad_loc + synthesis(grad_four_lat, lon_count, jnp.where(is_mean, 1.0, 0.5) * root_lon)
        grad_wmix = jnp.stack([gw_total[:, :, 0, :, 0] + gw_total[:, :, 1, :, 1], gw_total[:, :, 1, :, 0] - gw_total[:, :, 0, :, 1]], axis=-1)
        return grad_field, grad_wmix

    return jax.shard_map(local_step, mesh=mesh, in_specs=(field_spec, field_spec, P(), P(), P()), out_specs=(field_spec, P('member', None, None, None)), check_vma=False)
```

profile of v0, /device:TPU:0, one launch (start us, length us, event | category | flops | bytes accessed | tf_op | source)
XLA Modules:
  0.0 4335.5 jit_solution(16064400275864551772)
XLA Ops:
  25.6 59.7 %fusion.47 = f32[12,128,32,256]{1,3,2,0:T(8,128)} fusion(f32[12,128,32,256]{3,1,2,0:T(8,128)} %fusion.245), kind=kOutput, calls=%fused_computation.70 | convolution fusion | flops 38655033344 | bytes 100663296 | tf_op jit(solution)/shard_map/jit(fft)/dot.2 | solution.py:23
  85.2 83.0 %fusion.53 = f32[12,128,32,256]{1,3,2,0:T(8,128)} fusion(f32[12,128,32,256]{3,2,1,0:T(8,128)} %param.8, f32[256,256,1,1]{0,1,3,2:T(8,128)S(1)} %fusion.251), kind=kOutput, calls=%fused_computation.84 | convolution fusion | flops 38654705664 | bytes 100925440 | tf_op jit(solution)/shard_map/jit(fft)/dot.6 | solution.py:23
  168.3 82.6 %fusion.56 = f32[12,128,32,256]{1,3,2,0:T(8,128)} fusion(f32[12,128,32,256]{3,2,1,0:T(8,128)} %param.8, f32[256,256,1,1]{0,1,3,2:T(8,128)S(1)} %fusion.253), kind=kOutput, calls=%fused_computation.85 | convolution fusion | flops 38654705664 | bytes 100925440 | tf_op jit(solution)/shard_map/jit(fft)/dot.7 | solution.py:23
  289.7 56.8 %copy.82 = bf16[12,128,32,2,128]{1,2,0,3,4:T(8,128)(2,1)} copy(bf16[12,128,32,2,128]{1,4,2,0,3:T(8,128)(2,1)S(1)} %pad_maximum_fusion) | data formatting | bytes 50331648 | tf_op jit(solution)/shard_map/stack | solution.py:24
  403.9 224.7 %all-to-all-done = bf16[12,128,32,2,128]{1,2,0,3,4:T(8,128)(2,1)} async-done(((bf16[12,128,32,2,128]{1,2,0,3,4:T(8,128)(2,1)}), bf16[12,128,32,2,128]{1,2,0,3,4:T(8,128)(2,1)}, u32[]{:S(2)}, u32[]{:S(2)}) %all-to-all-start) | async-done | bytes 25165856 | tf_op jit(solution)/shard_map/all_to_all | solution.py:48
  655.6 41.5 convert_bitcast_fusion.3
  697.0 34.0 copy.121
  753.0 41.3 convert_bitcast_fusion.2
  794.3 61.6 %copy.91 = bf16[12,128,128,2,32]{1,3,0,4,2:T(2,128)(2,1)} copy(bf16[12,128,128,2,32]{2,1,3,0,4:T(8,128)(2,1)} %convert_bitcast_fusion.2) | data formatting | bytes 50331648 | tf_op jit(solution)/shard_map/convert_element_type | solution.py:51
  872.7 264.4 %all-to-all-done.1 = bf16[12,128,128,2,32]{1,3,0,4,2:T(2,128)(2,1)} async-done(((bf16[12,128,128,2,32]{1,3,0,4,2:T(2,128)(2,1)}), bf16[12,128,128,2,32]{1,3,0,4,2:T(2,128)(2,1)}, u32[]{:S(2)}, u32[]{:S(2)}) %all-to-all-start.1) | async-done | bytes 25165856 | tf_op jit(solution)/shard_map/all_to_all | solution.py:52
  1255.1 198.6 %reverse.8 = f32[12,128,32,127]{3,1,2,0:T(8,128)} reverse(f32[12,128,32,127]{3,1,2,0:T(8,128)} %slice.84), dimensions={3} | reverse | bytes 49938432 | tf_op jit(solution)/shard_map/jit(fft)/reverse | solution.py:30
  1472.8 198.6 %reverse.9 = f32[12,128,32,127]{3,1,2,0:T(8,128)} reverse(f32[12,128,32,127]{3,1,2,0:T(8,128)} %slice.85), dimensions={3} | reverse | bytes 49938432 | tf_op jit(solution)/shard_map/jit(fft)/reverse.1 | solution.py:30
  1689.0 48.5 %fusion.15 = f32[12,128,32,256]{3,1,2,0:T(8,128)} fusion(f32[12,128,32,128]{3,1,2,0:T(8,128)} %copy-done.1, f32[12,128,32,127]{3,1,2,0:T(8,128)} %reverse.8, f32[256,256,1,1]{1,0,3,2:T(8,128)S(1)} %fusion.237), kind=kOutput, calls=%fused_computation.26 | convolution fusion | flops 38692454400 | bytes 100728832 | tf_op jit(solution)/shard_map/jit(fft)/dot.4 | solution.py:30
  1737.4 48.3 %fusion.16 = f32[12,128,32,256]{3,1,2,0:T(8,128)} fusion(f32[12,128,32,128]{3,1,2,0:T(8,128)} %get-tuple-element.34, f32[12,128,32,127]{3,1,2,0:T(8,128)} %negate.4, f32[256,256,1,1]{1,0,3,2:T(8,128)S(1)} %copy-done.5), kind=kOutput, calls=%fused_computation.27 | convolution fusion | flops 38692454400 | bytes 100728832 | tf_op jit(solution)/shard_map/jit(fft)/dot.5 | solution.py:30
  1785.7 107.6 %fusion.4 = f32[12,128,32,256]{3,1,2,0:T(8,128)} fusion(f32[12,128,32,256]{3,1,2,0:T(8,128)} %fusion.16, f32[12,128,32,256]{3,1,2,0:T(8,128)} %fusion.15, f32[12,128,32,256]{3,2,1,0:T(8,128)} %param.9, f32[]{:T(128)S(6)} %multiply.91, f32[]{:T(128)S(6)} %multiply.89, f32[12,128,32,127]{3,1,2,0:T(8,128)} %reverse.8, f32[12,128,32,128]{3,1,2,0:T(8,128)} %copy-done.1, ...), kind=kOutput, calls=%fused_computation.12 | convolution fusion | flops 38906363904 | bytes 301858816 | tf_op jit(solution)/shard_map/jit(fft)/dot.3 | solution.py:30
  1893.4 54.0 %convolution_bitcast_fusion = f32[12,128,32,256]{1,3,2,0:T(8,128)} fusion(f32[12,128,32,256]{3,1,2,0:T(8,128)} %fusion.4, f32[256,256,1,1]{0,1,3,2:T(8,128)S(1)} %copy-done.4), kind=kOutput, calls=%fused_computation.82 | convolution fusion | flops 38654705664 | bytes 100925440 | tf_op jit(solution)/shard_map/jit(fft)/dot.7 | solution.py:23
  1947.4 54.0 %convolution_bitcast_fusion.1 = f32[12,128,32,256]{1,3,2,0:T(8,128)} fusion(f32[12,128,32,256]{3,1,2,0:T(8,128)} %fusion.4, f32[256,256,1,1]{0,1,3,2:T(8,128)S(1)} %copy-done.3), kind=kOutput, calls=%fused_computation.83 | convolution fusion | flops 38654705664 | bytes 100925440 | tf_op jit(solution)/shard_map/jit(fft)/dot.6 | solution.py:23
  2040.3 56.8 %copy.97 = bf16[12,128,32,2,128]{1,2,0,3,4:T(8,128)(2,1)} copy(bf16[12,128,32,2,128]{1,4,2,0,3:T(8,128)(2,1)S(1)} %pad_maximum_fusion.1) | data formatting | bytes 50331648 | tf_op jit(solution)/shard_map/stack | solution.py:24
  2106.0 31.6 copy.141
  2137.6 241.0 %all-to-all-done.2 = bf16[12,128,32,2,128]{1,2,0,3,4:T(8,128)(2,1)} async-done(((bf16[12,128,32,2,128]{1,2,0,3,4:T(8,128)(2,1)}), bf16[12,128,32,2,128]{1,2,0,3,4:T(8,128)(2,1)}, u32[]{:S(2)}, u32[]{:S(2)}) %all-to-all-start.2) | async-done | bytes 25165856 | tf_op jit(solution)/shard_map/all_to_all | solution.py:56
  2405.7 41.2 convert_bitcast_fusion.1
  2446.8 32.0 copy.140
  2478.8 34.1 copy.131
  2534.9 41.2 convert_bitcast_fusion
  2576.1 61.6 %copy.104 = bf16[12,128,128,2,32]{1,3,0,4,2:T(2,128)(2,1)} copy(bf16[12,128,128,2,32]{2,1,3,0,4:T(8,128)(2,1)} %convert_bitcast_fusion) | data formatting | bytes 50331648 | tf_op jit(solution)/shard_map/convert_element_type | solution.py:61
  2677.2 790.2 %all-reduce.7.cloned.1.call-done = f32[128,128,2,128,2]{3,1,4,2,0:T(8,128)} async-done(((f32[128,128,2,128,2]{3,1,4,2,0:T(8,128)}), f32[128,128,2,128,2]{3,1,4,2,0:T(8,128)}) %all-reduce.7.cloned.1.call-update) | async-done | bytes 33554448 | tf_op jit(solution)/shard_map/psum | solution.py:59
  3572.3 189.7 %reverse.10 = f32[12,128,32,127]{1,3,2,0:T(8,128)} reverse(f32[12,128,32,127]{1,3,2,0:T(8,128)} %slice.92), dimensions={3} | reverse | bytes 49938432 | tf_op jit(solution)/shard_map/jit(fft)/reverse | solution.py:30
  3779.8 189.7 %reverse.11 = f32[12,128,32,127]{1,3,2,0:T(8,128)} reverse(f32[12,128,32,127]{1,3,2,0:T(8,128)} %slice.93), dimensions={3} | reverse | bytes 49938432 | tf_op jit(solution)/shard_map/jit(fft)/reverse.1 | solution.py:30
  3987.1 86.5 %fusion.17 = f32[12,128,32,256]{3,1,2,0:T(8,128)} fusion(f32[12,128,32,128]{1,3,2,0:T(8,128)} %copy-done, f32[12,128,32,127]{1,3,2,0:T(8,128)} %reverse.10, f32[256,256,1,1]{1,0,3,2:T(8,128)S(1)} %copy-done.8), kind=kOutput, calls=%fused_computation.28 | convolution fusion | flops 38692454400 | bytes 100728832 | tf_op jit(solution)/shard_map/jit(fft)/dot.4 | solution.py:30
  4073.5 87.0 %fusion.18 = f32[12,128,32,256]{3,1,2,0:T(8,128)} fusion(f32[12,128,32,128]{1,3,2,0:T(8,128)} %get-tuple-element.32, f32[12,128,32,127]{1,3,2,0:T(8,128)} %negate.5, f32[256,256,1,1]{1,0,3,2:T(8,128)S(1)} %copy-done.7), kind=kOutput, calls=%fused_computation.29 | convolution fusion | flops 38692454400 | bytes 100728832 | tf_op jit(solution)/shard_map/jit(fft)/dot.5 | solution.py:30
  4160.5 122.1 %multiply_add_fusion = f32[12,128,32,256]{3,1,2,0:T(8,128)} fusion(f32[12,128,32,256]{3,1,2,0:T(8,128)} %fusion.18, f32[12,128,32,256]{3,1,2,0:T(8,128)} %fusion.17, f32[12,128,32,256]{3,2,1,0:T(8,128)} %param.9, f32[12,128,32,127]{1,3,2,0:T(8,128)} %reverse.10, f32[12,128,32,128]{1,3,2,0:T(8,128)} %copy-done, f32[12,128,32,127]{1,3,2,0:T(8,128)} %negate.5, ...), kind=kOutput, calls=%fused_computation.17 | convolution fusion | flops 38805962752 | bytes 301596672 | tf_op jit(solution)/shard_map/jit(fft)/dot.3 | solution.py:30
  4282.6 45.8 %copy.115 = f32[12,128,32,256]{3,2,1,0:T(8,128)} copy(f32[12,128,32,256]{3,1,2,0:T(8,128)} %multiply_add_fusion) | data formatting | bytes 100663296
  (73 shorter events, 611.5 us)
Async XLA Ops:
  346.5 282.0 %all-to-all-start = ((bf16[12,128,32,2,128]{1,2,0,3,4:T(8,128)(2,1)}), bf16[12,128,32,2,128]{1,2,0,3,4:T(8,128)(2,1)}, u32[]{:S(2)}, u32[]{:S(2)}) async-start(bf16[12,128,32,2,128]{1,2,0,3,4:T(8,128)(2,1)} %copy.82), calls=%async_computation | async-start | bytes 50331648 | tf_op jit(solution)/shard_map/all_to_all | solution.py:48
  375.4 3.3 copy-start.2
  855.9 281.2 %all-to-all-start.1 = ((bf16[12,128,128,2,32]{1,3,0,4,2:T(2,128)(2,1)}), bf16[12,128,128,2,32]{1,3,0,4,2:T(2,128)(2,1)}, u32[]{:S(2)}, u32[]{:S(2)}) async-start(bf16[12,128,128,2,32]{1,3,0,4,2:T(2,128)(2,1)} %copy.91), calls=%async_computation.1 | async-start | bytes 50331648 | tf_op jit(solution)/shard_map/all_to_all | solution.py:52
  1235.9 8.3 copy-start.1
  1689.0 48.5 %copy-start.5 = (f32[256,256,1,1]{1,0,3,2:T(8,128)S(1)}, f32[256,256,1,1]{1,0,3,2:T(8,128)}, u32[]{:S(2)}) copy-start(f32[256,256,1,1]{1,0,3,2:T(8,128)} %fusion.239) | copy-start | bytes 786436
  1737.4 48.3 %copy-start.6 = (f32[256,256,1,1]{1,0,3,2:T(8,128)S(1)}, f32[256,256,1,1]{1,0,3,2:T(8,128)}, u32[]{:S(2)}) copy-start(f32[256,256,1,1]{1,0,3,2:T(8,128)} %fusion.235) | copy-start | bytes 786436
  1785.7 107.6 %copy-start.4 = (f32[256,256,1,1]{0,1,3,2:T(8,128)S(1)}, f32[256,256,1,1]{0,1,3,2:T(8,128)}, u32[]{:S(2)}) copy-start(f32[256,256,1,1]{0,1,3,2:T(8,128)} %fusion.247) | copy-start | bytes 786436
  1893.4 54.0 %copy-start.3 = (f32[256,256,1,1]{0,1,3,2:T(8,128)S(1)}, f32[256,256,1,1]{0,1,3,2:T(8,128)}, u32[]{:S(2)}) copy-start(f32[256,256,1,1]{0,1,3,2:T(8,128)} %fusion.249) | copy-start | bytes 786436
  1947.4 54.0 %copy-start.10 = (f32[128]{0:T(128)S(1)}, f32[128]{0:T(128)}, u32[]{:S(2)}) copy-start(f32[128]{0:T(128)} %get-tuple-element.41) | copy-start | bytes 1540
  2097.1 281.5 %all-to-all-start.2 = ((bf16[12,128,32,2,128]{1,2,0,3,4:T(8,128)(2,1)}), bf16[12,128,32,2,128]{1,2,0,3,4:T(8,128)(2,1)}, u32[]{:S(2)}, u32[]{:S(2)}) async-start(bf16[12,128,32,2,128]{1,2,0,3,4:T(8,128)(2,1)} %copy.97), calls=%async_computation.2 | async-start | bytes 50331648 | tf_op jit(solution)/shard_map/all_to_all | solution.py:56
  2637.7 873.2 %all-to-all-start.3 = ((bf16[12,128,128,2,32]{1,3,0,4,2:T(2,128)(2,1)}), bf16[12,128,128,2,32]{1,3,0,4,2:T(2,128)(2,1)}, u32[]{:S(2)}, u32[]{:S(2)}) async-start(bf16[12,128,128,2,32]{1,3,0,4,2:T(2,128)(2,1)} %copy.104), calls=%async_computation.3 | async-start | bytes 50331648 | tf_op jit(solution)/shard_map/all_to_all | solution.py:62
  2646.1 821.2 %all-reduce.7.cloned.1.call-start = ((), (), s32[]{:S(2)}) async-start(), calls=%async_computation.4 | async-start | bytes 67108864 | tf_op jit(solution)/shard_map/psum | solution.py:59
  3526.1 9.0 copy-start.9
  3554.7 8.3 copy-start
  3969.5 17.6 copy-start.8
  3987.0 86.5 %copy-start.7 = (f32[256,256,1,1]{1,0,3,2:T(8,128)S(1)}, f32[256,256,1,1]{1,0,3,2:T(8,128)}, u32[]{:S(2)}) copy-start(f32[256,256,1,1]{1,0,3,2:T(8,128)} %fusion.243) | copy-start | bytes 786436
Sparse Core Ops, SparseCore 0:
  2673.9 793.3 all-reduce.6
where the time goes:
time: 4410 us; the launch traced here: 4340 us
  waiting for transfers between devices  1520 us (34%)
  local copies, waits for them, and re-layouts  1480 us (34%)
  matrix products  1070 us (24%)
  other arithmetic  221 us (5%)
    another operation x8, local copies, waits for them, and re-layouts, synthesis(): return jnp.fft.irfft(jnp.pad(complex_spec, pad_width), n=lon_count, axis=-1)  834 us
    psum x1, waiting for transfers between devices, local_step(): gw_total = lax.psum(gw_part, 'lat')  790 us
    another operation x6, matrix products, synthesis(): return jnp.fft.irfft(jnp.pad(complex_spec, pad_width), n=lon_count, axis=-1)  500 us
    another operation x5, matrix products, analysis(): spectrum = jnp.fft.rfft(values, axis=-1)[..., :mode_count] * mode_gains  333 us
    all_to_all x1, waiting for transfers between devices, local_step(): back_lat = lax.all_to_all(back_own, 'lat', 2, 4, tiled=True)  264 us
    all_to_all x1, waiting for transfers between devices, local_step(): grad_back_own = lax.all_to_all(grad_back_lat, 'lat', 4, 2, tiled=True)  241 us
    all_to_all x1, waiting for transfers between devices, local_step(): four_own = lax.all_to_all(four_lat, 'lat', 4, 2, tiled=True)  225 us
    another operation x2, local copies, waits for them, and re-layouts, analysis(): jnp.stack([spectrum.real, spectrum.imag], axis=-2).astype(jnp.bfloat16)  114 us
  transfers between devices with their start and end apart: 5, of which 4 were waited for; matrix products, arithmetic and copies ran while one was open for 4% of the time, Pallas kernels for 0%

commit v1 on v0

v1 whole, which is shorter than its diff:
```python
import functools
import math
import jax
import jax.numpy as jnp
import numpy as np
from jax import lax
from jax.experimental import pallas as pl
from jax.experimental.pallas import tpu as pltpu
from jax.sharding import PartitionSpec as P

BF16 = jnp.bfloat16
F32 = jnp.float32
LANES = 128
PAD = 8
VMEM_LIMIT = 60 * 1024 * 1024
NN = (((1,), (0,)), ((), ()))
NT = (((1,), (1,)), ((), ()))
TN = (((0,), (0,)), ((), ()))


def gelu_grad(values):
    cumulative = 0.5 * (1.0 + lax.erf(values * math.sqrt(0.5)))
    density = jnp.exp(-0.5 * values * values) * (1.0 / math.sqrt(2.0 * math.pi))
    return cumulative + values * density


def split(values):
    high = values.astype(BF16)
    low = (values - high.astype(F32)).astype(BF16)
    return high, low


def dot(lhs, rhs, dims):
    return lax.dot_general(lhs, rhs, dims, preferred_element_type=F32)


def fourier_rows(lon_count, mode_count, doubled):
    modes = np.arange(mode_count)[:, None]
    angle = 2.0 * np.pi * ((modes * np.arange(lon_count)[None, :]) % lon_count) / lon_count
    gain = np.where(modes == 0, 1.0, 2.0 if doubled else 1.0) / math.sqrt(lon_count)
    rows = np.concatenate([gain * np.cos(angle), -gain * np.sin(angle)], axis=0).astype(np.float32)
    high = rows.astype(BF16)
    low = (rows - high.astype(np.float32)).astype(BF16)
    return jnp.asarray(high), jnp.asarray(low)


def params():
    return pltpu.CompilerParams(vmem_limit_bytes=VMEM_LIMIT, dimension_semantics=("arbitrary",))


def cost(micros, bytes_accessed):
    return pl.CostEstimate(flops=int(micros * 1e6 * 200), bytes_accessed=int(bytes_accessed), transcendentals=0)


def load_rows(ref, pitch, rows_out, rows_in, source):
    def body(step, carry):
        for sub in range(8):
            row = step * 8 + sub
            ref[pl.ds(pl.multiple_of(row * pitch, 8), rows_in), :] = source(row)
        return carry
    lax.fori_loop(0, rows_out // 8, body, 0)


def analysis_tail(spec, half_refs, pitch, lat):
    for part in range(2):
        half_refs[part][pl.ds(pl.multiple_of(lat * pitch, 8), LANES), :] = spec[part * LANES:(part + 1) * LANES, :]


def emit_spectrum(out_ref, half_refs, pitch, dest_count, m_local, lat_local):
    def body(m_loc, carry):
        for dest in range(dest_count):
            for part in range(2):
                rows = half_refs[part][pl.ds(m_loc * dest_count + dest, lat_local, stride=pitch), :]
                out_ref[dest, 0, m_loc, :, part * LANES:(part + 1) * LANES] = rows.astype(BF16)
        return carry
    lax.fori_loop(0, m_local, body, 0, unroll=2)


def copy_field(field_ref, refs, pitch, lat_local):
    for half in range(2):
        load_rows(refs[half], pitch, LANES, lat_local,
                  lambda c, half=half: field_ref[0, c, :, half * LANES:(half + 1) * LANES])


def copy_spectrum(spec_ref, refs, pitch, dest_count, m_local, lat_local):
    def body(m_loc, carry):
        for src in range(dest_count):
            for part in range(2):
                refs[part][pl.ds(pl.multiple_of((m_loc * dest_count + src) * pitch, 8), lat_local), :] = (
                    spec_ref[src, 0, m_loc, :, part * LANES:(part + 1) * LANES].astype(F32))
        return carry
    lax.fori_loop(0, m_local, body, 0, unroll=2)


def analysis_kernel(field_ref, high_ref, low_ref, out_ref, f0, f1, s0, s1):
    dest_count, _, m_local, lat_local, _ = out_ref.shape
    pitch_t, pitch_m = lat_local + PAD, LANES + PAD
    copy_field(field_ref, (f0, f1), pitch_t, lat_local)

    def body(lat, carry):
        rows = jnp.concatenate([f0[pl.ds(lat, LANES, stride=pitch_t), :], f1[pl.ds(lat, LANES, stride=pitch_t), :]], axis=1)
        x_high, x_low = split(rows)
        spec = dot(high_ref[...], x_high, NT) + dot(low_ref[...], x_high, NT) + dot(high_ref[...], x_low, NT)
        analysis_tail(spec, (s0, s1), pitch_m, lat)
        return carry
    lax.fori_loop(0, lat_local, body, 0, unroll=2)
    emit_spectrum(out_ref, (s0, s1), pitch_m, dest_count, m_local, lat_local)


def middle_kernel(spec_ref, grad_ref, high_ref, low_ref, out_ref, g0, g1, f0, f1, s0, s1):
    dest_count, _, m_local, lat_local, _ = out_ref.shape
    pitch_t, pitch_m = lat_local + PAD, LANES + PAD
    copy_spectrum(spec_ref, (g0, g1), pitch_t, dest_count, m_local, lat_local)
    copy_field(grad_ref, (f0, f1), pitch_t, lat_local)

    def body(lat, carry):
        coef = jnp.concatenate([g0[pl.ds(lat, LANES, stride=pitch_t), :], g1[pl.ds(lat, LANES, stride=pitch_t), :]], axis=0).astype(BF16)
        hidden = dot(coef, high_ref[...], TN) + dot(coef, low_ref[...], TN)
        grad = jnp.concatenate([f0[pl.ds(lat, LANES, stride=pitch_t), :], f1[pl.ds(lat, LANES, stride=pitch_t), :]], axis=1)
        x_high, x_low = split(grad * gelu_grad(hidden))
        spec = dot(high_ref[...], x_high, NT) + dot(low_ref[...], x_high, NT) + dot(high_ref[...], x_low, NT)
        analysis_tail(spec, (s0, s1), pitch_m, lat)
        return carry
    lax.fori_loop(0, lat_local, body, 0, unroll=2)
    emit_spectrum(out_ref, (s0, s1), pitch_m, dest_count, m_local, lat_local)


def final_kernel(first, *refs):
    if first:
        spec_ref, grad_ref, high_ref, low_ref, out_ref, g0, g1, f0, f1 = refs
    else:
        spec_ref, grad_ref, high_ref, low_ref, _, out_ref, g0, g1, f0, f1 = refs
    dest_count, _, m_local, lat_local, _ = spec_ref.shape
    pitch_t = lat_local + PAD
    copy_spectrum(spec_ref, (g0, g1), pitch_t, dest_count, m_local, lat_local)

    def body(lat, carry):
        coef = jnp.concatenate([g0[pl.ds(lat, LANES, stride=pitch_t), :], g1[pl.ds(lat, LANES, stride=pitch_t), :]], axis=0).astype(BF16)
        wave = dot(coef, high_ref[...], TN) + dot(coef, low_ref[...], TN)
        f0[pl.ds(lat, LANES, stride=pitch_t), :] = wave[:, :LANES]
        f1[pl.ds(lat, LANES, stride=pitch_t), :] = wave[:, LANES:]
        return carry
    lax.fori_loop(0, lat_local, body, 0, unroll=2)

    def emit(step, carry):
        for sub in range(8):
            chan = step * 8 + sub
            for half, ref in enumerate((f0, f1)):
                cols = slice(half * LANES, (half + 1) * LANES)
                out_ref[0, chan, :, cols] = grad_ref[0, chan, :, cols] + ref[pl.ds(pl.multiple_of(chan * pitch_t, 8), lat_local), :]
        return carry
    lax.fori_loop(0, LANES // 8, emit, 0)


def legendre_kernel(spec_ref, poly_ref, out_ref, s0, s1):
    src_count, _, m_local, lat_local, _ = spec_ref.shape
    pitch = LANES + PAD

    def body(m_loc, carry):
        rows = jnp.concatenate([spec_ref[src, 0, m_loc] for src in range(src_count)], axis=0)
        coef = dot(poly_ref[m_loc], rows, NN)
        for part, ref in enumerate((s0, s1)):
            ref[pl.ds(pl.multiple_of(m_loc * pitch, 8), LANES), :] = coef[:, part * LANES:(part + 1) * LANES]
        return carry
    lax.fori_loop(0, m_local, body, 0, unroll=4)

    def emit(degree, carry):
        for part, ref in enumerate((s0, s1)):
            out_ref[degree, :, part * LANES:(part + 1) * LANES] = ref[pl.ds(degree, m_local, stride=pitch), :].astype(BF16)
        return carry
    lax.fori_loop(0, LANES, emit, 0, unroll=8)


def inverse_kernel(coef_ref, poly_ref, out_ref, s0, s1):
    dest_count, _, m_local, lat_local, _ = out_ref.shape
    pitch = m_local + PAD

    def fill(degree, carry):
        for part, ref in enumerate((s0, s1)):
            ref[pl.ds(pl.multiple_of(degree * pitch, 8), m_local), :] = coef_ref[degree, :, part * LANES:(part + 1) * LANES].astype(F32)
        return carry
    lax.fori_loop(0, LANES, fill, 0, unroll=8)

    def body(m_loc, carry):
        rows = jnp.concatenate([ref[pl.ds(m_loc, LANES, stride=pitch), :] for ref in (s0, s1)], axis=1).astype(BF16)
        back = dot(poly_ref[m_loc], rows, NN).astype(BF16)
        for dest in range(dest_count):
            out_ref[dest, 0, m_loc] = back[dest * lat_local:(dest + 1) * lat_local, :]
        return carry
    lax.fori_loop(0, m_local, body, 0, unroll=4)


def mix_kernel(coef_ref, mix_ref, out_ref):
    for k in range(coef_ref.shape[0]):
        out_ref[k] = dot(coef_ref[k], mix_ref[k], NT).astype(BF16)


def mixback_kernel(first, *refs):
    if first:
        dq_ref, coef_ref, mix_ref, out_ref, gw_ref = refs
    else:
        dq_ref, coef_ref, mix_ref, prev_ref, out_ref, gw_ref = refs
    for k in range(coef_ref.shape[0]):
        dq = dq_ref[k]
        coef = coef_ref[k]
        out_ref[k] = dot(dq, mix_ref[k], NN).astype(BF16)
        lhs = jnp.concatenate([dq[:, :LANES], dq[:, LANES:]], axis=0)
        rhs = jnp.concatenate([
            jnp.concatenate([coef[:, :LANES], -coef[:, LANES:]], axis=1),
            jnp.concatenate([coef[:, LANES:], coef[:, :LANES]], axis=1)], axis=0)
        grad = dot(lhs, rhs, TN)
        for part in range(2):
            piece = grad[:, part * LANES:(part + 1) * LANES]
            gw_ref[k, part] = piece if first else prev_ref[k, part] + piece


def solution(mesh):
    lat_size = mesh.shape['lat']
    field_spec = P('member', None, 'lat', None)
    chunk_count = 4

    def local_step(field_loc, grad_loc, p_fwd, p_inv, w_mix):
        batch, channels, lat_local, lon_count = field_loc.shape
        lat_count = p_fwd.shape[-1]
        m_local = lat_count // lat_size
        chunk = batch // chunk_count
        own = lax.axis_index('lat')
        d_high, d_low = fourier_rows(lon_count, lat_count, False)
        c_high, c_low = fourier_rows(lon_count, lat_count, True)

        def own_modes(poly):
            grouped = poly.reshape(m_local, lat_size, lat_count, lat_count)
            return lax.dynamic_index_in_dim(grouped, own, 1, keepdims=False).astype(BF16)

        pw_own, pi_own = own_modes(p_fwd), own_modes(p_inv)
        pw_back, pi_back = jnp.swapaxes(pw_own, 1, 2), jnp.swapaxes(pi_own, 1, 2)
        w_real, w_imag = w_mix[..., 0].astype(BF16), w_mix[..., 1].astype(BF16)
        w_big = jnp.concatenate([jnp.concatenate([w_real, -w_imag], axis=2), jnp.concatenate([w_imag, w_real], axis=2)], axis=1)

        spec_shape = jax.ShapeDtypeStruct((lat_size, chunk, m_local, lat_local, 2 * channels), BF16)
        coef_shape = jax.ShapeDtypeStruct((lat_count, chunk * m_local, 2 * channels), BF16)
        gw_shape = jax.ShapeDtypeStruct((lat_count, 2, channels, channels), F32)
        spec_block = pl.BlockSpec((lat_size, 1, m_local, lat_local, 2 * channels), lambda b: (0, b, 0, 0, 0))
        coef_block = pl.BlockSpec((lat_count, m_local, 2 * channels), lambda b: (0, b, 0))
        four_block = pl.BlockSpec((2 * lat_count, lon_count), lambda b: (0, 0))
        poly_block = pl.BlockSpec((m_local, lat_count, lat_count), lambda b: (0, 0, 0))

        def field_block(k):
            return pl.BlockSpec((1, channels, lat_local, lon_count), lambda b: (b + k * chunk, 0, 0, 0))

        fields = [pltpu.VMEM((channels * (lat_local + PAD), LANES), F32)] * 2
        spectra = [pltpu.VMEM((lat_count * (lat_local + PAD), LANES), F32)] * 2
        latspec = [pltpu.VMEM((lat_local * (lat_count + PAD), LANES), F32)] * 2
        legscr = [pltpu.VMEM((m_local * (lat_count + PAD), LANES), F32)] * 2
        invscr = [pltpu.VMEM((lat_count * (m_local + PAD), LANES), F32)] * 2
        mb = 1e6

        def analyse(k):
            return pl.pallas_call(analysis_kernel, grid=(chunk,), name="analyse", out_shape=spec_shape,
                                  in_specs=[field_block(k), four_block, four_block], out_specs=spec_block,
                                  scratch_shapes=fields + latspec, compiler_params=params(), cost_estimate=cost(20, 20 * mb))(field_loc, d_high, d_low)

        def middle(k, spec):
            return pl.pallas_call(middle_kernel, grid=(chunk,), name="middle", out_shape=spec_shape,
                                  in_specs=[spec_block, field_block(k), four_block, four_block], out_specs=spec_block,
                                  scratch_shapes=spectra + fields + latspec, compiler_params=params(), cost_estimate=cost(45, 26 * mb))(spec, grad_loc, c_high, c_low)

        def finish(k, spec, prev):
            first = prev is None
            extra = [] if first else [pl.BlockSpec(memory_space=pl.ANY)]
            args = [spec, grad_loc, d_high, d_low] + ([] if first else [prev])
            return pl.pallas_call(functools.partial(final_kernel, first), grid=(chunk,), name="finish",
                                  out_shape=jax.ShapeDtypeStruct(field_loc.shape, F32),
                                  in_specs=[spec_block, field_block(k), four_block, four_block] + extra, out_specs=field_block(k),
                                  input_output_aliases={} if first else {4: 0},
                                  scratch_shapes=spectra + fields, compiler_params=params(), cost_estimate=cost(20, 32 * mb))(*args)

        def legendre(spec, poly):
            return pl.pallas_call(legendre_kernel, grid=(chunk,), name="legendre", out_shape=coef_shape,
                                  in_specs=[spec_block, poly_block], out_specs=coef_block, scratch_shapes=legscr,
                                  compiler_params=params(), cost_estimate=cost(10, 14 * mb))(spec, poly)

        def inverse(coef, poly):
            return pl.pallas_call(inverse_kernel, grid=(chunk,), name="inverse", out_shape=spec_shape,
                                  in_specs=[coef_block, poly_block], out_specs=spec_block, scratch_shapes=invscr,
                                  compiler_params=params(), cost_estimate=cost(10, 14 * mb))(coef, poly)

        step_l = 8
        row_block = pl.BlockSpec((step_l, chunk * m_local, 2 * channels), lambda l: (l, 0, 0))
        mix_block = pl.BlockSpec((step_l, 2 * channels, 2 * channels), lambda l: (l, 0, 0))
        gw_block = pl.BlockSpec((step_l, 2, channels, channels), lambda l: (l, 0, 0, 0))

        def mix(coef):
            return pl.pallas_call(mix_kernel, grid=(lat_count // step_l,), name="mix", out_shape=coef_shape,
                                  in_specs=[row_block, mix_block], out_specs=row_block,
                                  compiler_params=params(), cost_estimate=cost(12, 30 * mb))(coef, w_big)

        def mixback(dq, coef, prev):
            first = prev is None
            args = [dq, coef, w_big] + ([] if first else [prev])
            return pl.pallas_call(functools.partial(mixback_kernel, first), grid=(lat_count // step_l,), name="mixback",
                                  out_shape=[coef_shape, gw_shape],
                                  in_specs=[row_block, row_block, mix_block] + ([] if first else [gw_block]), out_specs=[row_block, gw_block],
                                  input_output_aliases={} if first else {3: 1},
                                  compiler_params=params(), cost_estimate=cost(25, 70 * mb))(*args)

        def exchange(spec):
            return lax.all_to_all(spec, 'lat', 0, 0, tiled=True)

        def swap(values, bit):
            return lax.ppermute(values, 'lat', [(d, d ^ bit) for d in range(lat_size)])

        chunks = range(chunk_count)
        spec = [exchange(analyse(k)) for k in chunks]
        coef = [legendre(spec[k], pw_own) for k in chunks]
        spec = [exchange(inverse(mix(coef[k]), pi_back)) for k in chunks]
        spec = [exchange(middle(k, spec[k])) for k in chunks]
        gw = None
        out = []
        for k in chunks:
            dq = legendre(spec[k], pi_own)
            da, gw = mixback(dq, coef[k], gw)
            out.append(exchange(inverse(da, pw_back)))

        core, chip = own % 2, own // 2
        halves = gw.reshape(2, lat_count // 2, 2, channels, channels)
        half = lax.dynamic_index_in_dim(halves, core, 0, keepdims=False) + swap(lax.dynamic_index_in_dim(halves, 1 - core, 0, keepdims=False), 1)
        quarters = half.reshape(2, lat_count // 4, 2, channels, channels)
        quarter = lax.dynamic_index_in_dim(quarters, chip, 0, keepdims=False) + swap(lax.dynamic_index_in_dim(quarters, 1 - chip, 0, keepdims=False), 2)
        other = swap(quarter, 2)
        half = jnp.where(chip == 0, jnp.stack([quarter, other]), jnp.stack([other, quarter]))
        far = swap(half, 1)
        full = jnp.where(core == 0, jnp.stack([half, far]), jnp.stack([far, half])).reshape(lat_count, 2, channels, channels)
        grad_wmix = jnp.transpose(full, (0, 2, 3, 1))

        grad_field = None
        for k in chunks:
            grad_field = finish(k, out[k], grad_field)
        return grad_field, grad_wmix

    return jax.shard_map(local_step, mesh=mesh, in_specs=(field_spec, field_spec, P(), P(), P()), out_specs=(field_spec, P('member', None, None, None)), check_vma=False)
```

time: 4410 us -> 1550 us (0.35); the launches traced: 4340 us -> 1550 us
  local copies, waits for them, and re-layouts: 1480 us -> 43.3 us
  matrix products: 1070 us -> 0 us
  waiting for transfers between devices: 1520 us -> 662 us
  Pallas kernels: 0 us -> 706 us
  other arithmetic: 221 us -> 52.4 us
  starting transfers between devices: 34.7 us -> 86.7 us
    another operation x11 -> x0, local copies, waits for them, and re-layouts: 964 us -> none  [the longest x8 834 us: synthesis(): return jnp.fft.irfft(jnp.pad(complex_spec, pad_width), n=lon_count, axis=-1)]
    another operation x11 -> x0, matrix products: 833 us -> none  [the longest x6 500 us: synthesis(): return jnp.fft.irfft(jnp.pad(complex_spec, pad_width), n=lon_count, axis=-1)]
    psum x1 -> x0, waiting for transfers between devices: 790 us -> none  [local_step(): gw_total = lax.psum(gw_part, 'lat')]
    pallas_call x0 -> x36, Pallas kernels: none -> 706 us  [the longest x4 170 us: middle(): pl.pallas_call(middle_kernel, grid=(chunk,), name='middle', out_shape=spe...]
    convert_element_type x6 -> x3, local copies, waits for them, and re-layouts: 255 us -> 5.61 us  [the longest x2 4.41 us: own_modes(): lax.dynamic_index_in_dim(grouped, own, 1, keepdims=False).astype(BF16)]
    all_to_all x4 -> x16, waiting for transfers between devices: 730 us -> 493 us  [exchange(): return lax.all_to_all(spec, 'lat', 0, 0, tiled=True)]
    dot_general x7 -> x0, matrix products: 236 us -> none  [the longest x1 41.5 us: local_step(): jnp.einsum('mlt,bctrm->bclrm', pw_own, four_own, preferred_element_type=j...]
    ppermute x0 -> x4, waiting for transfers between devices: none -> 169 us  [swap(): return lax.ppermute(values, 'lat', [(d, d ^ bit) for d in range(lat_size)])]
  transfers between devices with their start and end apart: 5 -> 20, of which waited for: 4 -> 17; matrix products, arithmetic and copies ran while one was open for 4% -> 4% of each run, Pallas kernels for 0% -> 41%
where the time goes in v1:
time: 1550 us
  Pallas kernels  706 us (46%)
  waiting for transfers between devices  662 us (43%)
  starting transfers between devices  86.7 us (6%)
  other arithmetic  52.4 us (3%)
  local copies, waits for them, and re-layouts  43.3 us (3%)
    all_to_all x16, waiting for transfers between devices, exchange(): return lax.all_to_all(spec, 'lat', 0, 0, tiled=True)  493 us
    pallas_call x4, Pallas kernels, middle(): pl.pallas_call(middle_kernel, grid=(chunk,), name='middle', out_shape=spe...  170 us
    ppermute x4, waiting for transfers between devices, swap(): return lax.ppermute(values, 'lat', [(d, d ^ bit) for d in range(lat_size)])  169 us
    pallas_call x4, Pallas kernels, mixback(): pl.pallas_call(functools.partial(mixback_kernel, first), grid=(lat_count...  107 us
    pallas_call x4, Pallas kernels, analyse(): pl.pallas_call(analysis_kernel, grid=(chunk,), name='analyse', out_shape=...  102 us
    pallas_call x8, Pallas kernels, legendre(): pl.pallas_call(legendre_kernel, grid=(chunk,), name='legendre', out_shape...  90.1 us
    pallas_call x4, Pallas kernels, finish(): pl.pallas_call(functools.partial(final_kernel, first), grid=(chunk,), nam...  84.5 us
    all_to_all x16, starting transfers between devices, exchange(): return lax.all_to_all(spec, 'lat', 0, 0, tiled=True)  84.3 us
  transfers between devices with their start and end apart: 20, of which 17 were waited for; matrix products, arithmetic and copies ran while one was open for 4% of the time, Pallas kernels for 41%

profile of v1, /device:TPU:0, one launch (start us, length us, event | category | flops | bytes accessed | tf_op | source)
XLA Modules:
  0.0 1550.7 jit_solution(9012991583148187625)
XLA Ops:
  0.6 25.6 %analyse.5 = bf16[4,3,32,32,256]{4,3,2,1,0:T(8,128)(2,1)} custom-call(f32[12,128,32,256]{3,2,1,0:T(8,128)} %field_ref.7, bf16[256,256]{1,0:T(8,128)(2,1)} %constant.60.clone.high_ref.refs_2_, bf16[256,256]{1,0:T(8,128)(2,1)} %constant.61.clone.low_ref.refs_3_), custom_call_target="tpu_custom_call" | custom-call | flops 4000000000 | bytes 20000000 | tf_op jit(solution)/shard_map/analyse/pallas_call | solution.py:259
  31.5 25.6 %analyse.4 = bf16[4,3,32,32,256]{4,3,2,1,0:T(8,128)(2,1)} custom-call(f32[12,128,32,256]{3,2,1,0:T(8,128)} %field_ref.7, bf16[256,256]{1,0:T(8,128)(2,1)} %constant.60.clone.high_ref.refs_2_, bf16[256,256]{1,0:T(8,128)(2,1)} %constant.61.clone.low_ref.refs_3_), custom_call_target="tpu_custom_call" | custom-call | flops 4000000000 | bytes 20000000 | tf_op jit(solution)/shard_map/analyse/pallas_call | solution.py:259
  57.1 45.8 %all-to-all-done.3.spec_ref = bf16[4,3,32,32,256]{4,3,2,1,0:T(8,128)(2,1)} async-done(((bf16[4,3,32,32,256]{4,3,2,1,0:T(8,128)(2,1)}), bf16[4,3,32,32,256]{4,3,2,1,0:T(8,128)(2,1)}, u32[]{:S(2)}, u32[]{:S(2)}) %all-to-all-start.3) | async-done | bytes 6291488 | tf_op jit(solution)/shard_map/all_to_all | solution.py:308
  108.2 25.6 %analyse.7 = bf16[4,3,32,32,256]{4,3,2,1,0:T(8,128)(2,1)} custom-call(f32[12,128,32,256]{3,2,1,0:T(8,128)} %field_ref.7, bf16[256,256]{1,0:T(8,128)(2,1)} %constant.60.clone.high_ref.refs_2_, bf16[256,256]{1,0:T(8,128)(2,1)} %constant.61.clone.low_ref.refs_3_), custom_call_target="tpu_custom_call" | custom-call | flops 4000000000 | bytes 20000000 | tf_op jit(solution)/shard_map/analyse/pallas_call | solution.py:259
  133.8 44.7 %all-to-all-done.spec_ref = bf16[4,3,32,32,256]{4,3,2,1,0:T(8,128)(2,1)} async-done(((bf16[4,3,32,32,256]{4,3,2,1,0:T(8,128)(2,1)}), bf16[4,3,32,32,256]{4,3,2,1,0:T(8,128)(2,1)}, u32[]{:S(2)}, u32[]{:S(2)}) %all-to-all-start) | async-done | bytes 6291488 | tf_op jit(solution)/shard_map/all_to_all | solution.py:308
  183.8 25.6 %analyse.6 = bf16[4,3,32,32,256]{4,3,2,1,0:T(8,128)(2,1)} custom-call(f32[12,128,32,256]{3,2,1,0:T(8,128)} %field_ref.7, bf16[256,256]{1,0:T(8,128)(2,1)} %constant.60.clone.high_ref.refs_2_, bf16[256,256]{1,0:T(8,128)(2,1)} %constant.61.clone.low_ref.refs_3_), custom_call_target="tpu_custom_call" | custom-call | flops 4000000000 | bytes 20000000 | tf_op jit(solution)/shard_map/analyse/pallas_call | solution.py:259
  209.4 44.8 %all-to-all-done.9.spec_ref = bf16[4,3,32,32,256]{4,3,2,1,0:T(8,128)(2,1)} async-done(((bf16[4,3,32,32,256]{4,3,2,1,0:T(8,128)(2,1)}), bf16[4,3,32,32,256]{4,3,2,1,0:T(8,128)(2,1)}, u32[]{:S(2)}, u32[]{:S(2)}) %all-to-all-start.9) | async-done | bytes 6291488 | tf_op jit(solution)/shard_map/all_to_all | solution.py:308
  295.9 17.6 %mix.7.coef_ref = bf16[128,96,256]{2,1,0:T(8,128)(2,1)} custom-call(bf16[128,96,256]{2,1,0:T(8,128)(2,1)} %legendre.14.coef_ref.refs_1_, bf16[128,256,256]{2,1,0:T(8,128)(2,1)} %maximum_maximum_fusion.mix_ref.refs_2_), custom_call_target="tpu_custom_call" | custom-call | flops 2400000000 | bytes 30000000 | tf_op jit(solution)/shard_map/mix/pallas_call | solution.py:294
  373.9 31.4 %all-to-all-done.10.spec_ref = bf16[4,3,32,32,256]{4,3,2,1,0:T(8,128)(2,1)} async-done(((bf16[4,3,32,32,256]{4,3,2,1,0:T(8,128)(2,1)}), bf16[4,3,32,32,256]{4,3,2,1,0:T(8,128)(2,1)}, u32[]{:S(2)}, u32[]{:S(2)}) %all-to-all-start.10) | async-done | bytes 6291488 | tf_op jit(solution)/shard_map/all_to_all | solution.py:308
  449.6 31.3 %all-to-all-done.7.spec_ref = bf16[4,3,32,32,256]{4,3,2,1,0:T(8,128)(2,1)} async-done(((bf16[4,3,32,32,256]{4,3,2,1,0:T(8,128)(2,1)}), bf16[4,3,32,32,256]{4,3,2,1,0:T(8,128)(2,1)}, u32[]{:S(2)}, u32[]{:S(2)}) %all-to-all-start.7) | async-done | bytes 6291488 | tf_op jit(solution)/shard_map/all_to_all | solution.py:308
  525.1 31.5 %all-to-all-done.4.spec_ref = bf16[4,3,32,32,256]{4,3,2,1,0:T(8,128)(2,1)} async-done(((bf16[4,3,32,32,256]{4,3,2,1,0:T(8,128)(2,1)}), bf16[4,3,32,32,256]{4,3,2,1,0:T(8,128)(2,1)}, u32[]{:S(2)}, u32[]{:S(2)}) %all-to-all-start.4) | async-done | bytes 6291488 | tf_op jit(solution)/shard_map/all_to_all | solution.py:308
  561.8 42.6 %middle.7 = bf16[4,3,32,32,256]{4,3,2,1,0:T(8,128)(2,1)} custom-call(bf16[4,3,32,32,256]{4,3,2,1,0:T(8,128)(2,1)} %all-to-all-done.10.spec_ref, f32[12,128,32,256]{3,2,1,0:T(8,128)} %refs_1_.7, bf16[256,256]{1,0:T(8,128)(2,1)} %constant.62.clone.high_ref, bf16[256,256]{1,0:T(8,128)(2,1)} %constant.63.clone.low_ref), custom_call_target="tpu_custom_call" | custom-call | flops 8999999488 | bytes 26000000 | tf_op jit(solution)/shard_map/middle/pallas_call | solution.py:264
  604.3 27.8 %all-to-all-done.1.spec_ref = bf16[4,3,32,32,256]{4,3,2,1,0:T(8,128)(2,1)} async-done(((bf16[4,3,32,32,256]{4,3,2,1,0:T(8,128)(2,1)}), bf16[4,3,32,32,256]{4,3,2,1,0:T(8,128)(2,1)}, u32[]{:S(2)}, u32[]{:S(2)}) %all-to-all-start.1) | async-done | bytes 6291488 | tf_op jit(solution)/shard_map/all_to_all | solution.py:308
  637.4 42.6 %middle.6 = bf16[4,3,32,32,256]{4,3,2,1,0:T(8,128)(2,1)} custom-call(bf16[4,3,32,32,256]{4,3,2,1,0:T(8,128)(2,1)} %all-to-all-done.7.spec_ref, f32[12,128,32,256]{3,2,1,0:T(8,128)} %refs_1_.7, bf16[256,256]{1,0:T(8,128)(2,1)} %constant.62.clone.high_ref, bf16[256,256]{1,0:T(8,128)(2,1)} %constant.63.clone.low_ref), custom_call_target="tpu_custom_call" | custom-call | flops 8999999488 | bytes 26000000 | tf_op jit(solution)/shard_map/middle/pallas_call | solution.py:264
  680.0 27.8 %all-to-all-done.11.spec_ref = bf16[4,3,32,32,256]{4,3,2,1,0:T(8,128)(2,1)} async-done(((bf16[4,3,32,32,256]{4,3,2,1,0:T(8,128)(2,1)}), bf16[4,3,32,32,256]{4,3,2,1,0:T(8,128)(2,1)}, u32[]{:S(2)}, u32[]{:S(2)}) %all-to-all-start.11) | async-done | bytes 6291488 | tf_op jit(solution)/shard_map/all_to_all | solution.py:308
  713.2 42.6 %middle.5 = bf16[4,3,32,32,256]{4,3,2,1,0:T(8,128)(2,1)} custom-call(bf16[4,3,32,32,256]{4,3,2,1,0:T(8,128)(2,1)} %all-to-all-done.4.spec_ref, f32[12,128,32,256]{3,2,1,0:T(8,128)} %refs_1_.7, bf16[256,256]{1,0:T(8,128)(2,1)} %constant.62.clone.high_ref, bf16[256,256]{1,0:T(8,128)(2,1)} %constant.63.clone.low_ref), custom_call_target="tpu_custom_call" | custom-call | flops 8999999488 | bytes 26000000 | tf_op jit(solution)/shard_map/middle/pallas_call | solution.py:264
  755.8 27.6 %all-to-all-done.8.spec_ref = bf16[4,3,32,32,256]{4,3,2,1,0:T(8,128)(2,1)} async-done(((bf16[4,3,32,32,256]{4,3,2,1,0:T(8,128)(2,1)}), bf16[4,3,32,32,256]{4,3,2,1,0:T(8,128)(2,1)}, u32[]{:S(2)}, u32[]{:S(2)}) %all-to-all-start.8) | async-done | bytes 6291488 | tf_op jit(solution)/shard_map/all_to_all | solution.py:308
  788.6 42.6 %middle.4 = bf16[4,3,32,32,256]{4,3,2,1,0:T(8,128)(2,1)} custom-call(bf16[4,3,32,32,256]{4,3,2,1,0:T(8,128)(2,1)} %all-to-all-done.1.spec_ref, f32[12,128,32,256]{3,2,1,0:T(8,128)} %refs_1_.7, bf16[256,256]{1,0:T(8,128)(2,1)} %constant.62.clone.high_ref, bf16[256,256]{1,0:T(8,128)(2,1)} %constant.63.clone.low_ref), custom_call_target="tpu_custom_call" | custom-call | flops 8999999488 | bytes 26000000 | tf_op jit(solution)/shard_map/middle/pallas_call | solution.py:264
  831.2 27.8 %all-to-all-done.5.spec_ref = bf16[4,3,32,32,256]{4,3,2,1,0:T(8,128)(2,1)} async-done(((bf16[4,3,32,32,256]{4,3,2,1,0:T(8,128)(2,1)}), bf16[4,3,32,32,256]{4,3,2,1,0:T(8,128)(2,1)}, u32[]{:S(2)}, u32[]{:S(2)}) %all-to-all-start.5) | async-done | bytes 6291488 | tf_op jit(solution)/shard_map/all_to_all | solution.py:308
  898.0 24.3 %mixback.4 = (bf16[128,96,256]{2,1,0:T(8,128)(2,1)}, f32[128,2,128,128]{3,2,1,0:T(8,128)}) custom-call(bf16[128,96,256]{2,1,0:T(8,128)(2,1)} %legendre.15.refs_0_, bf16[128,96,256]{2,1,0:T(8,128)(2,1)} %legendre.14.coef_ref.refs_1_, bf16[128,256,256]{2,1,0:T(8,128)(2,1)} %maximum_maximum_fusion.mix_ref.refs_2_), custom_call_target="tpu_custom_call" | custom-call | flops 5000000000 | bytes 70000000 | tf_op jit(solution)/shard_map/mixback/pallas_call | solution.py:301
  922.4 27.6 %mixback.5 = (bf16[128,96,256]{2,1,0:T(8,128)(2,1)}, f32[128,2,128,128]{3,2,1,0:T(8,128)}) custom-call(bf16[128,96,256]{2,1,0:T(8,128)(2,1)} %legendre.13.refs_0_, bf16[128,96,256]{2,1,0:T(8,128)(2,1)} %legendre.12.coef_ref.refs_1_, bf16[128,256,256]{2,1,0:T(8,128)(2,1)} %maximum_maximum_fusion.mix_ref.refs_2_, ...), custom_call_target="tpu_custom_call", output_to_operand_aliasing={{1}: (3, {})} | custom-call | flops 5000000000 | bytes 70000000 | tf_op jit(solution)/shard_map/mixback/pallas_call | solution.py:301
  949.9 27.6 %mixback.6 = (bf16[128,96,256]{2,1,0:T(8,128)(2,1)}, f32[128,2,128,128]{3,2,1,0:T(8,128)}) custom-call(bf16[128,96,256]{2,1,0:T(8,128)(2,1)} %legendre.11.refs_0_, bf16[128,96,256]{2,1,0:T(8,128)(2,1)} %legendre.10.coef_ref.refs_1_, bf16[128,256,256]{2,1,0:T(8,128)(2,1)} %maximum_maximum_fusion.mix_ref.refs_2_, ...), custom_call_target="tpu_custom_call", output_to_operand_aliasing={{1}: (3, {})} | custom-call | flops 5000000000 | bytes 70000000 | tf_op jit(solution)/shard_map/mixback/pallas_call | solution.py:301
  988.7 27.5 %mixback.7 = (bf16[128,96,256]{2,1,0:T(8,128)(2,1)}, f32[128,2,128,128]{3,2,1,0:T(8,128)}) custom-call(bf16[128,96,256]{2,1,0:T(8,128)(2,1)} %legendre.9.refs_0_, bf16[128,96,256]{2,1,0:T(8,128)(2,1)} %legendre.8.coef_ref.refs_1_, bf16[128,256,256]{2,1,0:T(8,128)(2,1)} %maximum_maximum_fusion.mix_ref.refs_2_, ...), custom_call_target="tpu_custom_call", output_to_operand_aliasing={{1}: (3, {})} | custom-call | flops 5000000000 | bytes 70000000 | tf_op jit(solution)/shard_map/mixback/pallas_call | solution.py:301
  1068.7 42.2 %all-to-all-done.13.refs_0_ = bf16[4,3,32,32,256]{4,3,2,1,0:T(8,128)(2,1)} async-done(((bf16[4,3,32,32,256]{4,3,2,1,0:T(8,128)(2,1)}), bf16[4,3,32,32,256]{4,3,2,1,0:T(8,128)(2,1)}, u32[]{:S(2)}, u32[]{:S(2)}) %all-to-all-start.13) | async-done | bytes 6291488 | tf_op jit(solution)/shard_map/all_to_all | solution.py:308
  1116.1 84.6 %collective-permute-done.1 = f32[32,2,128,128]{3,2,1,0:T(8,128)} collective-permute-done((f32[32,2,128,128]{3,2,1,0:T(8,128)}, f32[32,2,128,128]{3,2,1,0:T(8,128)}, u32[]{:S(2)}, u32[]{:S(2)}) %collective-permute-start.1) | collective-permute-done | bytes 4194336 | tf_op jit(solution)/shard_map/ppermute | solution.py:311
  1217.6 50.6 %all-to-all-done.15.refs_0_ = bf16[4,3,32,32,256]{4,3,2,1,0:T(8,128)(2,1)} async-done(((bf16[4,3,32,32,256]{4,3,2,1,0:T(8,128)(2,1)}), bf16[4,3,32,32,256]{4,3,2,1,0:T(8,128)(2,1)}, u32[]{:S(2)}, u32[]{:S(2)}) %all-to-all-start.15) | async-done | bytes 6291488 | tf_op jit(solution)/shard_map/all_to_all | solution.py:308
  1273.4 84.6 %collective-permute-done.2 = f32[32,2,128,128]{3,2,1,0:T(8,128)} collective-permute-done((f32[32,2,128,128]{3,2,1,0:T(8,128)}, f32[32,2,128,128]{3,2,1,0:T(8,128)}, u32[]{:S(2)}, u32[]{:S(2)}) %collective-permute-start.2) | collective-permute-done | bytes 4194336 | tf_op jit(solution)/shard_map/ppermute | solution.py:311
  1378.6 46.4 %all-to-all-done.14.refs_0_ = bf16[4,3,32,32,256]{4,3,2,1,0:T(8,128)(2,1)} async-done(((bf16[4,3,32,32,256]{4,3,2,1,0:T(8,128)(2,1)}), bf16[4,3,32,32,256]{4,3,2,1,0:T(8,128)(2,1)}, u32[]{:S(2)}, u32[]{:S(2)}) %all-to-all-start.14) | async-done | bytes 6291488 | tf_op jit(solution)/shard_map/all_to_all | solution.py:308
  1430.4 21.1 %finish.4.refs_4_ = f32[12,128,32,256]{3,2,1,0:T(8,128)} custom-call(bf16[4,3,32,32,256]{4,3,2,1,0:T(8,128)(2,1)} %all-to-all-done.15.refs_0_, f32[12,128,32,256]{3,2,1,0:T(8,128)} %refs_1_.7, bf16[256,256]{1,0:T(8,128)(2,1)} %constant.60.clone.high_ref.refs_2_, bf16[256,256]{1,0:T(8,128)(2,1)} %constant.61.clone.low_ref.refs_3_), custom_call_target="tpu_custom_call" | custom-call | flops 4000000000 | bytes 32000000 | tf_op jit(solution)/shard_map/finish/pallas_call | solution.py:272
  1451.5 21.1 %finish.5.refs_4_ = f32[12,128,32,256]{3,2,1,0:T(8,128)} custom-call(bf16[4,3,32,32,256]{4,3,2,1,0:T(8,128)(2,1)} %all-to-all-done.14.refs_0_, f32[12,128,32,256]{3,2,1,0:T(8,128)} %refs_1_.7, bf16[256,256]{1,0:T(8,128)(2,1)} %constant.60.clone.high_ref.refs_2_, bf16[256,256]{1,0:T(8,128)(2,1)} %constant.61.clone.low_ref.refs_3_, ...), custom_call_target="tpu_custom_call", output_to_operand_aliasing={{}: (4, {})} | custom-call | flops 4000000000 | bytes 32000000 | tf_op jit(solution)/shard_map/finish/pallas_call | solution.py:272
  1472.6 21.1 %finish.6.refs_4_ = f32[12,128,32,256]{3,2,1,0:T(8,128)} custom-call(bf16[4,3,32,32,256]{4,3,2,1,0:T(8,128)(2,1)} %all-to-all-done.13.refs_0_, f32[12,128,32,256]{3,2,1,0:T(8,128)} %refs_1_.7, bf16[256,256]{1,0:T(8,128)(2,1)} %constant.60.clone.high_ref.refs_2_, bf16[256,256]{1,0:T(8,128)(2,1)} %constant.61.clone.low_ref.refs_3_, ...), custom_call_target="tpu_custom_call", output_to_operand_aliasing={{}: (4, {})} | custom-call | flops 4000000000 | bytes 32000000 | tf_op jit(solution)/shard_map/finish/pallas_call | solution.py:272
  1500.5 21.1 %finish.7 = f32[12,128,32,256]{3,2,1,0:T(8,128)} custom-call(bf16[4,3,32,32,256]{4,3,2,1,0:T(8,128)(2,1)} %all-to-all-done.12.refs_0_, f32[12,128,32,256]{3,2,1,0:T(8,128)} %refs_1_.7, bf16[256,256]{1,0:T(8,128)(2,1)} %constant.60.clone.high_ref.refs_2_, bf16[256,256]{1,0:T(8,128)(2,1)} %constant.61.clone.low_ref.refs_3_, ...), custom_call_target="tpu_custom_call", output_to_operand_aliasing={{}: (4, {})} | custom-call | flops 4000000000 | bytes 32000000 | tf_op jit(solution)/shard_map/finish/pallas_call | solution.py:272
  (63 shorter events, 419.0 us)
Async XLA Ops:
  26.2 76.7 %all-to-all-start.3 = ((bf16[4,3,32,32,256]{4,3,2,1,0:T(8,128)(2,1)}), bf16[4,3,32,32,256]{4,3,2,1,0:T(8,128)(2,1)}, u32[]{:S(2)}, u32[]{:S(2)}) async-start(bf16[4,3,32,32,256]{4,3,2,1,0:T(8,128)(2,1)} %analyse.5), calls=%async_computation.3 | async-start | bytes 12582912 | tf_op jit(solution)/shard_map/all_to_all | solution.py:308
  102.9 75.6 %all-to-all-start = ((bf16[4,3,32,32,256]{4,3,2,1,0:T(8,128)(2,1)}), bf16[4,3,32,32,256]{4,3,2,1,0:T(8,128)(2,1)}, u32[]{:S(2)}, u32[]{:S(2)}) async-start(bf16[4,3,32,32,256]{4,3,2,1,0:T(8,128)(2,1)} %analyse.4), calls=%async_computation | async-start | bytes 12582912 | tf_op jit(solution)/shard_map/all_to_all | solution.py:308
  178.5 75.6 %all-to-all-start.9 = ((bf16[4,3,32,32,256]{4,3,2,1,0:T(8,128)(2,1)}), bf16[4,3,32,32,256]{4,3,2,1,0:T(8,128)(2,1)}, u32[]{:S(2)}, u32[]{:S(2)}) async-start(bf16[4,3,32,32,256]{4,3,2,1,0:T(8,128)(2,1)} %analyse.7), calls=%async_computation.9 | async-start | bytes 12582912 | tf_op jit(solution)/shard_map/all_to_all | solution.py:308
  254.1 75.6 %all-to-all-start.6 = ((bf16[4,3,32,32,256]{4,3,2,1,0:T(8,128)(2,1)}), bf16[4,3,32,32,256]{4,3,2,1,0:T(8,128)(2,1)}, u32[]{:S(2)}, u32[]{:S(2)}) async-start(bf16[4,3,32,32,256]{4,3,2,1,0:T(8,128)(2,1)} %analyse.6), calls=%async_computation.6 | async-start | bytes 12582912 | tf_op jit(solution)/shard_map/all_to_all | solution.py:308
  261.8 13.8 copy-start
  329.7 75.6 %all-to-all-start.10 = ((bf16[4,3,32,32,256]{4,3,2,1,0:T(8,128)(2,1)}), bf16[4,3,32,32,256]{4,3,2,1,0:T(8,128)(2,1)}, u32[]{:S(2)}, u32[]{:S(2)}) async-start(bf16[4,3,32,32,256]{4,3,2,1,0:T(8,128)(2,1)} %inverse.11), calls=%async_computation.10 | async-start | bytes 12582912 | tf_op jit(solution)/shard_map/all_to_all | solution.py:308
  405.3 75.6 %all-to-all-start.7 = ((bf16[4,3,32,32,256]{4,3,2,1,0:T(8,128)(2,1)}), bf16[4,3,32,32,256]{4,3,2,1,0:T(8,128)(2,1)}, u32[]{:S(2)}, u32[]{:S(2)}) async-start(bf16[4,3,32,32,256]{4,3,2,1,0:T(8,128)(2,1)} %inverse.10), calls=%async_computation.7 | async-start | bytes 12582912 | tf_op jit(solution)/shard_map/all_to_all | solution.py:308
  480.9 75.6 %all-to-all-start.4 = ((bf16[4,3,32,32,256]{4,3,2,1,0:T(8,128)(2,1)}), bf16[4,3,32,32,256]{4,3,2,1,0:T(8,128)(2,1)}, u32[]{:S(2)}, u32[]{:S(2)}) async-start(bf16[4,3,32,32,256]{4,3,2,1,0:T(8,128)(2,1)} %inverse.9), calls=%async_computation.4 | async-start | bytes 12582912 | tf_op jit(solution)/shard_map/all_to_all | solution.py:308
  556.5 75.6 %all-to-all-start.1 = ((bf16[4,3,32,32,256]{4,3,2,1,0:T(8,128)(2,1)}), bf16[4,3,32,32,256]{4,3,2,1,0:T(8,128)(2,1)}, u32[]{:S(2)}, u32[]{:S(2)}) async-start(bf16[4,3,32,32,256]{4,3,2,1,0:T(8,128)(2,1)} %inverse.8), calls=%async_computation.1 | async-start | bytes 12582912 | tf_op jit(solution)/shard_map/all_to_all | solution.py:308
  632.1 75.6 %all-to-all-start.11 = ((bf16[4,3,32,32,256]{4,3,2,1,0:T(8,128)(2,1)}), bf16[4,3,32,32,256]{4,3,2,1,0:T(8,128)(2,1)}, u32[]{:S(2)}, u32[]{:S(2)}) async-start(bf16[4,3,32,32,256]{4,3,2,1,0:T(8,128)(2,1)} %middle.7), calls=%async_computation.11 | async-start | bytes 12582912 | tf_op jit(solution)/shard_map/all_to_all | solution.py:308
  707.7 75.6 %all-to-all-start.8 = ((bf16[4,3,32,32,256]{4,3,2,1,0:T(8,128)(2,1)}), bf16[4,3,32,32,256]{4,3,2,1,0:T(8,128)(2,1)}, u32[]{:S(2)}, u32[]{:S(2)}) async-start(bf16[4,3,32,32,256]{4,3,2,1,0:T(8,128)(2,1)} %middle.6), calls=%async_computation.8 | async-start | bytes 12582912 | tf_op jit(solution)/shard_map/all_to_all | solution.py:308
  783.4 75.6 %all-to-all-start.5 = ((bf16[4,3,32,32,256]{4,3,2,1,0:T(8,128)(2,1)}), bf16[4,3,32,32,256]{4,3,2,1,0:T(8,128)(2,1)}, u32[]{:S(2)}, u32[]{:S(2)}) async-start(bf16[4,3,32,32,256]{4,3,2,1,0:T(8,128)(2,1)} %middle.5), calls=%async_computation.5 | async-start | bytes 12582912 | tf_op jit(solution)/shard_map/all_to_all | solution.py:308
  859.0 118.5 %all-to-all-start.2 = ((bf16[4,3,32,32,256]{4,3,2,1,0:T(8,128)(2,1)}), bf16[4,3,32,32,256]{4,3,2,1,0:T(8,128)(2,1)}, u32[]{:S(2)}, u32[]{:S(2)}) async-start(bf16[4,3,32,32,256]{4,3,2,1,0:T(8,128)(2,1)} %middle.4), calls=%async_computation.2 | async-start | bytes 12582912 | tf_op jit(solution)/shard_map/all_to_all | solution.py:308
  1024.2 15.8 %collective-permute-start = (f32[64,2,128,128]{3,2,1,0:T(8,128)}, f32[64,2,128,128]{3,2,1,0:T(8,128)}, u32[]{:S(2)}, u32[]{:S(2)}) collective-permute-start(f32[64,2,128,128]{3,2,1,0:T(8,128)} %dynamic-slice_bitcast_fusion), channel_id=1, source_target_pairs={{0,1},{1,0},{2,3},{3,2},{4,5},{5,4},{6,7},{7,6}} | collective-permute-start | bytes 25165832 | tf_op jit(solution)/shard_map/ppermute | solution.py:311
  1034.7 76.2 %all-to-all-start.13 = ((bf16[4,3,32,32,256]{4,3,2,1,0:T(8,128)(2,1)}), bf16[4,3,32,32,256]{4,3,2,1,0:T(8,128)(2,1)}, u32[]{:S(2)}, u32[]{:S(2)}) async-start(bf16[4,3,32,32,256]{4,3,2,1,0:T(8,128)(2,1)} %inverse.13), calls=%async_computation.13 | async-start | bytes 12582912 | tf_op jit(solution)/shard_map/all_to_all | solution.py:308
  1056.6 144.2 %collective-permute-start.1 = (f32[32,2,128,128]{3,2,1,0:T(8,128)}, f32[32,2,128,128]{3,2,1,0:T(8,128)}, u32[]{:S(2)}, u32[]{:S(2)}) collective-permute-start(f32[32,2,128,128]{3,2,1,0:T(8,128)} %dynamic-slice_bitcast_fusion.1), channel_id=1, source_target_pairs={{0,2},{1,3},{2,0},{3,1},{4,6},{5,7},{6,4},{7,5}} | collective-permute-start | bytes 12582920 | tf_op jit(solution)/shard_map/ppermute | solution.py:311
  1110.9 157.3 %all-to-all-start.15 = ((bf16[4,3,32,32,256]{4,3,2,1,0:T(8,128)(2,1)}), bf16[4,3,32,32,256]{4,3,2,1,0:T(8,128)(2,1)}, u32[]{:S(2)}, u32[]{:S(2)}) async-start(bf16[4,3,32,32,256]{4,3,2,1,0:T(8,128)(2,1)} %inverse.15), calls=%async_computation.15 | async-start | bytes 12582912 | tf_op jit(solution)/shard_map/all_to_all | solution.py:308
  1207.4 150.7 %collective-permute-start.2 = (f32[32,2,128,128]{3,2,1,0:T(8,128)}, f32[32,2,128,128]{3,2,1,0:T(8,128)}, u32[]{:S(2)}, u32[]{:S(2)}) collective-permute-start(f32[32,2,128,128]{3,2,1,0:T(8,128)} %bitcast_add_fusion.1), channel_id=1, source_target_pairs={{0,2},{1,3},{2,0},{3,1},{4,6},{5,7},{6,4},{7,5}} | collective-permute-start | bytes 12582920 | tf_op jit(solution)/shard_map/ppermute | solution.py:311
  1268.2 156.7 %all-to-all-start.14 = ((bf16[4,3,32,32,256]{4,3,2,1,0:T(8,128)(2,1)}), bf16[4,3,32,32,256]{4,3,2,1,0:T(8,128)(2,1)}, u32[]{:S(2)}, u32[]{:S(2)}) async-start(bf16[4,3,32,32,256]{4,3,2,1,0:T(8,128)(2,1)} %inverse.14), calls=%async_computation.14 | async-start | bytes 12582912 | tf_op jit(solution)/shard_map/all_to_all | solution.py:308
  1368.4 160.6 %collective-permute-start.3 = (f32[2,32,2,128,128]{4,3,2,1,0:T(8,128)}, f32[2,32,2,128,128]{4,3,2,1,0:T(8,128)}, u32[]{:S(2)}, u32[]{:S(2)}) collective-permute-start(f32[2,32,2,128,128]{4,3,2,1,0:T(8,128)} %maximum_select_fusion.2), channel_id=1, source_target_pairs={{0,1},{1,0},{2,3},{3,2},{4,5},{5,4},{6,7},{7,6}} | collective-permute-start | bytes 25165832 | tf_op jit(solution)/shard_map/ppermute | solution.py:311
  1424.9 75.6 %all-to-all-start.12 = ((bf16[4,3,32,32,256]{4,3,2,1,0:T(8,128)(2,1)}), bf16[4,3,32,32,256]{4,3,2,1,0:T(8,128)(2,1)}, u32[]{:S(2)}, u32[]{:S(2)}) async-start(bf16[4,3,32,32,256]{4,3,2,1,0:T(8,128)(2,1)} %inverse.12), calls=%async_computation.12 | async-start | bytes 12582912 | tf_op jit(solution)/shard_map/all_to_all | solution.py:308
